TPU v7x, 256 devices: a whole 4x4x8 slice. The times are simulated.
256 devices in a mesh: dp: 128 (over y, x_lo, z, core), rep: 2 (over x_hi).
Axes of the slice: x: 4 (x_hi: 2, x_lo: 2; x = x_hi * 2 + x_lo), y: 4, z: 8, core: 2. Of those that a mesh axis runs over, the one named last changes fastest.
Arguments:
- gate_pre: bfloat16 [2, 16384, 5632], P(None, 'dp', 'rep'), may hold values from -8 to 8
- up_pre: bfloat16 [2, 16384, 5632], P(None, 'dp', 'rep'), may hold values from -6 to 6
- out_grad: bfloat16 [2, 16384, 1024], P(None, 'dp'), may hold values from -24 to 24
- master: float32 [1024, 5632], P('dp', 'rep'), may hold values from -0.078125 to 0.078125
- moment_one: float32 [1024, 5632], P('dp', 'rep'), may hold values from -0.02 to 0.02
- moment_two: float32 [1024, 5632], P('dp', 'rep'), may hold values from 1e-06 to 1e-05
Outputs:
- layer_out: bfloat16 [2, 16384, 1024], P(None, 'dp', 'rep')
- gate_grad: bfloat16 [2, 16384, 5632], P(None, 'dp', 'rep')
- up_grad: bfloat16 [2, 16384, 5632], P(None, 'dp', 'rep')
- master_new: float32 [1024, 5632], P('dp', 'rep')
- moment_one_new: float32 [1024, 5632], P('dp', 'rep')
- moment_two_new: float32 [1024, 5632], P('dp', 'rep')
All inputs are finite; a program needn't handle non-finite values.
Results may differ from a plain program's by a relative error of at most 0.0048.
The roundings to bfloat16 on the way count: a program that leaves them out, or rounds other values in their place, can miss the bound.
Values may be sent and summed in bfloat16 or wider, within the bound.
A program may use at most 128 MiB of HBM per device.

v0:
```python
import jax
import jax.numpy as jnp
from jax import lax
from jax.sharding import Mesh
from jax.sharding import PartitionSpec as P

DP = ("dp_0", "dp_1", "dp_2", "dp_3")
first_power = 2.6561398887587544e-05
second_power = 0.005920529220333997


def in_blocks(x, dim, peers):
    before, after = (x.shape[:dim], x.shape[dim + 1 :])
    return jnp.moveaxis(x.reshape(*before, peers, -1, *after), dim, 0)


def sent_and_summed(x, axis, dim):
    peers = lax.axis_size(axis)
    parts = lax.all_to_all(in_blocks(x, dim, peers), axis, 0, 0, tiled=True)
    return jnp.sum(parts, axis=0)


def sum_by_chip_2(x, chips, core, dim):
    sizes = (lax.axis_size(chips), lax.axis_size(core))
    parts = in_blocks(x, dim, sizes[0] * sizes[1])
    inside = parts.shape[1:]
    parts = parts.reshape(*sizes, *inside).swapaxes(0, 1).reshape(-1, *inside)
    parts = lax.psum_scatter(parts, core, scatter_dimension=0, tiled=True)
    return lax.psum_scatter(parts, chips, scatter_dimension=0, tiled=True)[0]


def grad_rows(cotangent, hidden):
    return lax.dot_general(
        cotangent, hidden, (((0,), (0,)), ((), ())), preferred_element_type=jnp.float32
    )


def on_device(gate_pre, up_pre, out_grad, master, moment_one, moment_two):
    shard_bf = master.astype(jnp.bfloat16)
    weights = lax.all_gather(shard_bf, DP, axis=0, tiled=True)
    micro = gate_pre.shape[0]
    total = micro * gate_pre.shape[1] * lax.axis_size(DP)
    own_rows = master.shape[0]
    outs_list = []
    gate_list = []
    up_list = []
    hidden_list = []
    grad_sum = None
    for index in range(micro):
        gate = gate_pre[index].astype(jnp.float32)
        up_val = up_pre[index].astype(jnp.float32)
        sig = jax.nn.sigmoid(gate)
        hidden = (gate * sig * up_val).astype(jnp.bfloat16)
        hidden_list.append(hidden)
        partial_out = lax.dot_general(
            hidden, weights, (((1,), (1,)), ((), ())), preferred_element_type=jnp.float32
        )
        outs_list.append(sent_and_summed(partial_out, "rep", 1).astype(jnp.bfloat16))
        hid_grad = jnp.dot(out_grad[index], weights, preferred_element_type=jnp.float32)
        gate_list.append(
            (hid_grad * up_val * sig * (1.0 + gate * (1.0 - sig))).astype(jnp.bfloat16)
        )
        up_list.append((hid_grad * gate * sig).astype(jnp.bfloat16))

        def single_term(start, count, cotangent=out_grad[index], current=hidden):
            return grad_rows(cotangent, current)

        shard_grad = sum_by_chip_2(
            single_term(
                jnp.int32(0),
                own_rows * lax.axis_size(("dp_0", "dp_1", "dp_2")) * lax.axis_size("dp_3"),
            ),
            ("dp_0", "dp_1", "dp_2"),
            "dp_3",
            0,
        )
        grad_sum = shard_grad if grad_sum is None else grad_sum + shard_grad
    main_grad = grad_sum / jnp.float32(total)
    first = 0.9 * moment_one + 0.1 * main_grad
    second = 0.95 * moment_two + 0.05 * main_grad * main_grad
    update = first / (1.0 - first_power) / (jnp.sqrt(second / (1.0 - second_power)) + 1e-08)
    master_new = master - 0.003 * (update + 0.1 * master)
    return (
        jnp.stack(outs_list),
        jnp.stack(gate_list),
        jnp.stack(up_list),
        master_new,
        first,
        second,
    )


def solution(mesh):
    torus = Mesh(
        mesh.devices.reshape(4, 2, 8, 2, mesh.shape["rep"]), ("dp_0", "dp_1", "dp_2", "dp_3", "rep")
    )
    return jax.shard_map(
        on_device,
        mesh=torus,
        in_specs=(
            P(None, DP, "rep"),
            P(None, DP, "rep"),
            P(None, DP, None),
            P(DP, "rep"),
            P(DP, "rep"),
            P(DP, "rep"),
        ),
        out_specs=(
            P(None, DP, "rep"),
            P(None, DP, "rep"),
            P(None, DP, "rep"),
            P(DP, "rep"),
            P(DP, "rep"),
            P(DP, "rep"),
        ),
        check_vma=False,
    )
```

profile of v0, /device:TPU:32, one launch (start us, length us, event | category | flops | bytes accessed | tf_op | source)
XLA Modules:
  0.0 641.3 jit_solution(1135383162872716029)
XLA Ops:
  7.2 0.0 reduce-scatter.5.cloned.1.call-start
  7.2 3.2 fusion.37
  10.5 6.0 convolution_add_fusion
  16.5 9.5 %copy.12 = f32[2,64,8,2816]{3,2,1,0:T(8,128)} copy(f32[2,64,8,2816]{3,2,0,1:T(8,128)} %bitcast.143) | data formatting | bytes 23068672 | tf_op jit(solution)/shard_map/add | solution.py:77
  26.0 0.0 reduce-scatter.5.cloned.1.call-update
  26.0 0.0 reduce-scatter.3.cloned.1.call-start
  26.1 27.0 %reduce-scatter.5.cloned.1.call-done = f32[64,8,2816]{2,1,0:T(8,128)} async-done(((f32[128,8,2816]{2,1,0:T(8,128)}), f32[64,8,2816]{2,1,0:T(8,128)}) %reduce-scatter.5.cloned.1.call-update) | async-done | bytes 5767184 | tf_op jit(solution)/shard_map/reduce_scatter | solution.py:28
  53.1 0.0 all-gather.2.cloned.1.call-start
  53.1 329.1 %reduce-scatter.3.cloned.1.call-done = f32[1,8,2816]{2,1,0:T(8,128)} async-done(((f32[64,8,2816]{2,1,0:T(8,128)}), f32[1,8,2816]{2,1,0:T(8,128)}) %reduce-scatter.3.cloned.1.call-update) | async-done | bytes 90128 | tf_op jit(solution)/shard_map/reduce_scatter | solution.py:29
  382.3 1.6 multiply_subtract_fusion
  383.9 0.0 all-gather.2.cloned.1.call-update
  384.0 216.6 %all-gather.2.cloned.1.call-done = bf16[1024,2816]{1,0:T(8,128)(2,1)} async-done(((bf16[8,2816]{1,0:T(8,128)(2,1)}), bf16[1024,2816]{1,0:T(8,128)(2,1)}) %all-gather.2.cloned.1.call-update) | async-done | bytes 5767184 | tf_op jit(solution)/shard_map/all_gather | solution.py:40
  600.5 5.4 convolution_bitcast_fusion
  605.9 4.3 all-to-all-start.1
  610.2 3.8 fusion.44
  614.0 0.1 slice-done.1
  614.2 0.4 copy-done.2
  614.6 0.1 copy-done.4
  614.7 3.1 fusion.40
  617.8 2.8 convolution_bitcast_fusion.1
  620.6 4.9 all-to-all-start
  625.5 3.4 pad_maximum_fusion
  628.9 5.0 all-to-all-done
  634.0 0.7 pad_maximum_fusion.2
  (24 shorter events, 0.1 us)
Async XLA Ops:
  7.2 3.3 copy-start
  7.2 3.3 copy-start.1
  7.2 3.3 copy-start.3
  7.2 45.9 %reduce-scatter.5.cloned.1.call-start = ((), (), s32[]{:S(2)}) async-start(), calls=%async_computation.6 | async-start | bytes 17301504 | tf_op jit(solution)/shard_map/reduce_scatter | solution.py:28
  26.0 356.2 %reduce-scatter.3.cloned.1.call-start = ((), (), s32[]{:S(2)}) async-start(), calls=%async_computation.5 | async-start | bytes 5857280 | tf_op jit(solution)/shard_map/reduce_scatter | solution.py:29
  53.1 329.2 %copy-start.6 = (f32[8,2816]{1,0:T(8,128)S(1)}, f32[8,2816]{1,0:T(8,128)}, u32[]{:S(2)}) copy-start(f32[8,2816]{1,0:T(8,128)} %param.9) | copy-start | bytes 270340
  53.1 329.2 %copy-start.7 = (f32[8,2816]{1,0:T(8,128)S(1)}, f32[8,2816]{1,0:T(8,128)}, u32[]{:S(2)}) copy-start(f32[8,2816]{1,0:T(8,128)} %param.10) | copy-start | bytes 270340
  53.1 329.2 %copy-start.8 = (f32[8,2816]{1,0:T(8,128)S(1)}, f32[8,2816]{1,0:T(8,128)}, u32[]{:S(2)}) copy-start(f32[8,2816]{1,0:T(8,128)} %param.11) | copy-start | bytes 270340
  53.1 547.4 %all-gather.2.cloned.1.call-start = ((), (), s32[]{:S(2)}) async-start(), calls=%async_computation.4 | async-start | bytes 5812224 | tf_op jit(solution)/shard_map/all_gather | solution.py:40
  605.9 8.1 %slice-start = ((s8[5767168]{0:T(1024)(128)(4,1)}), s8[1572864]{0:T(1024)(128)(4,1)S(1)}, s32[]{:S(2)}) async-start(s8[5767168]{0:T(1024)(128)(4,1)} %bitcast.146), calls=%async_computation.7 | async-start | bytes 3145728
  605.9 14.6 %all-to-all-start.1 = ((f32[2,128,512]{2,1,0:T(8,128)}), f32[2,128,512]{2,1,0:T(8,128)S(1)}, u32[]{:S(2)}, u32[]{:S(2)}) async-start(f32[2,128,512]{2,1,0:T(8,128)} %convolution_bitcast_fusion), calls=%async_computation.1 | async-start | bytes 1048576 | tf_op jit(solution)/shard_map/all_to_all | solution.py:19
  610.2 3.9 slice-start.1
  610.2 4.4 copy-start.2
  610.2 4.5 copy-start.4
  620.6 4.9 copy-start.5
  620.6 13.4 %all-to-all-start = ((f32[2,128,512]{2,1,0:T(8,128)}), f32[2,128,512]{2,1,0:T(8,128)S(1)}, u32[]{:S(2)}, u32[]{:S(2)}) async-start(f32[2,128,512]{2,1,0:T(8,128)} %convolution_bitcast_fusion.1), calls=%async_computation | async-start | bytes 1048576 | tf_op jit(solution)/shard_map/all_to_all | solution.py:19
Sparse Core Ops, SparseCore 0:
  26.2 26.8 reduce-scatter.4
  55.6 326.6 reduce-scatter.2
  384.7 215.7 all-gather.1
where the time goes:
time: 642 us; the launch traced here: 641 us
  waiting for transfers between devices  578 us (90%)
  matrix products  24.3 us (4%)
  between operations  13.8 us (2%)
  local copies, waits for them, and re-layouts  10.2 us (2%)
  starting transfers between devices  9.33 us (1%)
    reduce_scatter x1, waiting for transfers between devices, sum_by_chip_2(): return lax.psum_scatter(parts, chips, scatter_dimension=0, tiled=True)[0]  329 us
    all_gather x1, waiting for transfers between devices, on_device(): weights = lax.all_gather(shard_bf, DP, axis=0, tiled=True)  217 us
    reduce_scatter x1, waiting for transfers between devices, sum_by_chip_2(): parts = lax.psum_scatter(parts, core, scatter_dimension=0, tiled=True)  27 us
  transfers between devices with their start and end apart: 5, of which 4 were waited for; matrix products, arithmetic and copies ran while one was open for 2% of the time, Pallas kernels for 0%

commit v1 on v0

--- a/solution.py
+++ b/solution.py
@@ -37,7 +37,9 @@
 
 def on_device(gate_pre, up_pre, out_grad, master, moment_one, moment_two):
     shard_bf = master.astype(jnp.bfloat16)
-    weights = lax.all_gather(shard_bf, DP, axis=0, tiled=True)
+    weights = jnp.concatenate(
+        lax.all_to_all(jnp.stack([shard_bf] * lax.axis_size(DP)), DP, 0, 0), axis=0
+    )
     micro = gate_pre.shape[0]
     total = micro * gate_pre.shape[1] * lax.axis_size(DP)
     own_rows = master.shape[0]

time: 642 us -> 566 us (0.88)
  waiting for transfers between devices: 578 us -> 361 us
  blocking collectives: 0 us -> 141 us
    all_gather x1 -> x0, waiting for transfers between devices: 217 us -> none  [on_device(): weights = lax.all_gather(shard_bf, DP, axis=0, tiled=True)]
    all_to_all x0 -> x1, blocking collectives: none -> 141 us  [on_device(): lax.all_to_all(jnp.stack([shard_bf] * lax.axis_size(DP)), DP, 0, 0)]
  transfers between devices with their start and end apart: 5 -> 4, of which waited for: 4 -> 3; matrix products, arithmetic and copies ran while one was open for 2% -> 2% of each run, Pallas kernels for 0% -> 0%
where the time goes in v1:
time: 566 us
  waiting for transfers between devices  361 us (64%)
  blocking collectives  141 us (25%)
  matrix products  21.7 us (4%)
  between operations  14.1 us (2%)
  local copies, waits for them, and re-layouts  13.1 us (2%)
  starting transfers between devices  9.12 us (2%)
  other arithmetic  5.81 us (1%)
    reduce_scatter x1, waiting for transfers between devices, sum_by_chip_2(): return lax.psum_scatter(parts, chips, scatter_dimension=0, tiled=True)[0]  329 us
    all_to_all x1, blocking collectives, on_device(): lax.all_to_all(jnp.stack([shard_bf] * lax.axis_size(DP)), DP, 0, 0)  141 us
    reduce_scatter x1, waiting for transfers between devices, sum_by_chip_2(): parts = lax.psum_scatter(parts, core, scatter_dimension=0, tiled=True)  27 us
  transfers between devices with their start and end apart: 4, of which 3 were waited for; matrix products, arithmetic and copies ran while one was open for 2% of the time, Pallas kernels for 0%

profile of v1, /device:TPU:32, one launch (start us, length us, event | category | flops | bytes accessed | tf_op | source)
XLA Modules:
  0.0 566.0 jit_solution(6935990033090908916)
XLA Ops:
  7.2 0.0 reduce-scatter.5.cloned.1.call-start
  7.2 3.2 fusion.41
  10.5 6.0 %convolution_add_fusion = f32[2816,1024]{0,1:T(8,128)} fusion(f32[2816,1024]{0,1:T(8,128)S(1)} %fusion.41, bf16[2,128,1024]{2,1,0:T(8,128)(2,1)S(1)} %copy-done.4, bf16[2,128,2816]{2,1,0:T(8,128)(2,1)S(1)} %copy-done.1, bf16[2,128,2816]{2,1,0:T(8,128)(2,1)S(1)} %copy-done.2), kind=kOutput, calls=%fused_computation | convolution fusion | flops 743964672 | bytes 24772608 | tf_op jit(solution)/shard_map/dot_general | solution.py:33
  16.5 9.5 %copy.12 = f32[2,64,8,2816]{3,2,1,0:T(8,128)} copy(f32[2,64,8,2816]{3,2,0,1:T(8,128)} %bitcast.148) | data formatting | bytes 23068672 | tf_op jit(solution)/shard_map/add | solution.py:79
  26.0 0.0 reduce-scatter.5.cloned.1.call-update
  26.0 0.0 reduce-scatter.3.cloned.1.call-start
  26.1 27.0 %reduce-scatter.5.cloned.1.call-done = f32[64,8,2816]{2,1,0:T(8,128)} async-done(((f32[128,8,2816]{2,1,0:T(8,128)}), f32[64,8,2816]{2,1,0:T(8,128)}) %reduce-scatter.5.cloned.1.call-update) | async-done | bytes 5767184 | tf_op jit(solution)/shard_map/reduce_scatter | solution.py:28
  53.1 329.2 %reduce-scatter.3.cloned.1.call-done = f32[1,8,2816]{2,1,0:T(8,128)} async-done(((f32[64,8,2816]{2,1,0:T(8,128)}), f32[1,8,2816]{2,1,0:T(8,128)}) %reduce-scatter.3.cloned.1.call-update) | async-done | bytes 90128 | tf_op jit(solution)/shard_map/reduce_scatter | solution.py:29
  382.3 1.6 multiply_subtract_fusion
  383.9 0.4 stack.16
  384.3 141.4 %all_to_all.15 = bf16[128,8,2816]{2,1,0:T(8,128)(2,1)S(1)} all-to-all(bf16[128,8,2816]{2,1,0:T(8,128)(2,1)S(1)} %stack.16), channel_id=1, replica_groups=mesh['dp_0'=4,'dp_1'=2,'dp_2'=8,'dp_3'=2,'rep'=2] {'dp_0','dp_1','dp_2',..., dimensions={0} | all-to-all | bytes 11534336 | tf_op jit(solution)/shard_map/all_to_all | solution.py:41
  525.7 2.5 copy-done
  528.1 2.8 convolution_bitcast_fusion
  530.9 4.1 all-to-all-start.2
  535.1 3.8 fusion
  538.9 0.1 slice-done.1
  539.0 0.4 copy-done.3
  539.4 0.1 copy-done.5
  539.5 3.1 fusion.44
  542.6 2.8 convolution_bitcast_fusion.1
  545.4 4.9 all-to-all-start.1
  550.3 3.4 pad_maximum_fusion
  553.7 4.7 all-to-all-done.1
  558.4 0.7 pad_maximum_fusion.2
  (25 shorter events, 0.1 us)
Async XLA Ops:
  7.2 3.3 copy-start.1
  7.2 3.3 copy-start.2
  7.2 3.3 copy-start.4
  7.2 45.9 %reduce-scatter.5.cloned.1.call-start = ((), (), s32[]{:S(2)}) async-start(), calls=%async_computation.6 | async-start | bytes 17301504 | tf_op jit(solution)/shard_map/reduce_scatter | solution.py:28
  26.0 356.2 %reduce-scatter.3.cloned.1.call-start = ((), (), s32[]{:S(2)}) async-start(), calls=%async_computation.5 | async-start | bytes 5857280 | tf_op jit(solution)/shard_map/reduce_scatter | solution.py:29
  53.1 329.2 %copy-start.7 = (f32[8,2816]{1,0:T(8,128)S(1)}, f32[8,2816]{1,0:T(8,128)}, u32[]{:S(2)}) copy-start(f32[8,2816]{1,0:T(8,128)} %param.9) | copy-start | bytes 270340
  53.1 329.2 %copy-start.8 = (f32[8,2816]{1,0:T(8,128)S(1)}, f32[8,2816]{1,0:T(8,128)}, u32[]{:S(2)}) copy-start(f32[8,2816]{1,0:T(8,128)} %param.10) | copy-start | bytes 270340
  53.1 329.2 %copy-start.9 = (f32[8,2816]{1,0:T(8,128)S(1)}, f32[8,2816]{1,0:T(8,128)}, u32[]{:S(2)}) copy-start(f32[8,2816]{1,0:T(8,128)} %param.11) | copy-start | bytes 270340
  525.7 2.5 copy-start
  530.9 7.9 %slice-start = ((s8[5767168]{0:T(1024)(128)(4,1)}), s8[1572864]{0:T(1024)(128)(4,1)S(1)}, s32[]{:S(2)}) async-start(s8[5767168]{0:T(1024)(128)(4,1)} %bitcast.151), calls=%async_computation.7 | async-start | bytes 3145728
  530.9 14.5 %all-to-all-start.2 = ((f32[2,128,512]{2,1,0:T(8,128)}), f32[2,128,512]{2,1,0:T(8,128)S(1)}, u32[]{:S(2)}, u32[]{:S(2)}) async-start(f32[2,128,512]{2,1,0:T(8,128)} %convolution_bitcast_fusion), calls=%async_computation.2 | async-start | bytes 1048576 | tf_op jit(solution)/shard_map/all_to_all | solution.py:19
  535.1 3.9 slice-start.1
  535.1 4.4 copy-start.3
  535.1 4.5 copy-start.5
  545.4 4.9 copy-start.6
  545.4 13.0 %all-to-all-start.1 = ((f32[2,128,512]{2,1,0:T(8,128)}), f32[2,128,512]{2,1,0:T(8,128)S(1)}, u32[]{:S(2)}, u32[]{:S(2)}) async-start(f32[2,128,512]{2,1,0:T(8,128)} %convolution_bitcast_fusion.1), calls=%async_computation.1 | async-start | bytes 1048576 | tf_op jit(solution)/shard_map/all_to_all | solution.py:19
Sparse Core Ops, SparseCore 0:
  26.2 26.8 reduce-scatter.4
  55.6 326.6 reduce-scatter.2
